TPU v7x, 32 devices: a whole 2x2x4 slice. The times are simulated.
32 devices in a mesh: dp: 4 (over y, x), expert: 8 (over z, core).
Axes of the slice: x: 2, y: 2, z: 4, core: 2. Of those that a mesh axis runs over, the one named last changes fastest.
Arguments:
- grad_out: bfloat16 [4096, 3072], P(('dp', 'expert')), may hold values from -6 to 6
- expert_ids: int32 [4096, 2], P(('dp', 'expert')), may hold values from 0 to 7, all different within a row; in each aligned block of 128 rows (0 to 127, 128 to 255, ...) at most 36 rows name the same one
- down_weight: bfloat16 [8, 1024, 3072], P('expert'), may hold values from -0.109375 to 0.109375
- history_grad: float32 [8, 8], replicated, may hold values from 0.5 to 3
- history_hidden: float32 [8, 8], replicated, may hold values from 0.5 to 3
Outputs:
- hidden_scaled: bfloat16 [4, 8, 288, 1024], P('dp', 'expert')
- new_history_grad: float32 [8, 8], replicated
- new_history_hidden: float32 [8, 8], replicated
Inputs may be any that keep to these rules, and one draw needn't show every extreme that they name: `expert_ids`: each row names 2 different experts; among the 128 rows of one device no expert is named more than 36 times, a bound that some block reaches in some devices.
All inputs are finite; a program needn't handle non-finite values.
Results may differ from a plain program's by a relative error of at most 0.0045.
Values may be sent and summed in bfloat16 or wider, within the bound.
A program may use at most 128 MiB of HBM per device.

v0:
```python
import functools

import jax
import jax.numpy as jnp
from jax import lax
from jax.experimental import pallas as pl
from jax.experimental.pallas import tpu as pltpu
from jax.sharding import PartitionSpec as P

MESH = pl.DeviceIdType.MESH
PARTS = 4
LANES = 128


def flip_bits(q, k, count):
    out, bit = 0, 1
    while bit < count:
        a, b = (q // bit) % 2, (k // bit) % 2
        out = out + bit * (a + b - 2 * a * b)
        bit *= 2
    return out


def kernel(
    n_dp, n_exp, experts, capacity,
    grad_hbm, ids_ref, hist_g_ref, hist_h_ref, weight_hbm,
    out_ref, best_ref,
    grad_ref, held, weight, send, send_rest, recv, recv_rest, rest_rows, slots, mine, peaks_in,
    grad_sem, weight_sem, send_sem, recv_sem, send_rest_sem, recv_rest_sem, peak_send_sem, peak_recv_sem,
):
    tokens = grad_ref.shape[0]
    main = send.shape[1]
    slices = n_exp // experts
    chips = n_exp // 2
    my_dp, me = lax.axis_index("dp"), lax.axis_index("expert")
    q0, c0 = me // 2, me % 2
    partner = q0 * 2 + 1 - c0
    own = me // slices
    grad_load = pltpu.make_async_copy(grad_hbm, grad_ref, grad_sem)
    grad_load.start()
    load = pltpu.make_async_copy(weight_hbm.at[0], weight, weight_sem)

    barrier = pltpu.get_barrier_semaphore()

    everyone = n_dp * n_exp
    here = my_dp * n_exp + me

    def greet(j, x):
        peer = (here + j) % everyone
        pl.semaphore_signal(
            barrier, inc=1, device_id=(peer // n_exp, peer % n_exp), device_id_type=MESH
        )
        return x

    lax.fori_loop(1, everyone, greet, 0)

    expert_row = lax.broadcasted_iota(jnp.int32, (LANES, tokens), 0)
    ids = ids_ref[...]
    mask_t = jnp.where((ids[0:1, :] == expert_row) | (ids[1:2, :] == expert_row), 1.0, 0.0)
    row = lax.broadcasted_iota(jnp.int32, (tokens, tokens), 0)
    col = lax.broadcasted_iota(jnp.int32, (tokens, tokens), 1)
    earlier = jnp.where(row < col, 1.0, 0.0).astype(jnp.bfloat16)
    before = jnp.dot(mask_t.astype(jnp.bfloat16), earlier, preferred_element_type=jnp.float32)
    slots[...] = jnp.where(mask_t > 0.5, before, -1.0)
    scale_in = 1.0 / jnp.max(hist_g_ref[...], axis=0, keepdims=True)
    scale_hidden = 1.0 / jnp.max(hist_h_ref[...], axis=0, keepdims=True)
    which = lax.broadcasted_iota(jnp.int32, (1, experts), 1)

    def pick(values, e):
        return jnp.sum(jnp.where(which == e, values, 0.0), axis=1, keepdims=True)

    position = lax.broadcasted_iota(jnp.int32, (capacity, tokens), 0).astype(jnp.float32)

    def prepare(e):
        onehot = jnp.where(slots[pl.ds(e, 1), :] == position, 1.0, 0.0).astype(jnp.bfloat16)
        rows = jnp.dot(onehot, grad_ref[...], preferred_element_type=jnp.float32)
        block = jnp.clip(rows * pick(scale_in, e), -1.0, 1.0)
        send[e] = block[0:main].astype(jnp.bfloat16)
        send_rest[e] = block[main:capacity].astype(jnp.bfloat16)

    span = weight.shape[1] // PARTS

    def outgoing(d, p):
        columns = pl.ds(p * span, span)
        return pltpu.make_async_remote_copy(
            src_ref=send.at[d // slices, :, columns], dst_ref=recv.at[me, :, columns],
            send_sem=send_sem.at[p, d], recv_sem=recv_sem.at[p, me],
            device_id=(my_dp, d), device_id_type=MESH,
        )

    def outgoing_rest(d):
        return pltpu.make_async_remote_copy(
            src_ref=send_rest.at[d // slices], dst_ref=recv_rest.at[me],
            send_sem=send_rest_sem.at[d], recv_sem=recv_rest_sem.at[me],
            device_id=(my_dp, d), device_id_type=MESH,
        )

    def incoming(s, p):
        columns = pl.ds(p * span, span)
        return pltpu.make_async_remote_copy(
            src_ref=send.at[0, :, columns], dst_ref=recv.at[s, :, columns],
            send_sem=send_sem.at[p, s], recv_sem=recv_sem.at[p, s],
            device_id=(my_dp, s), device_id_type=MESH,
        )

    def incoming_rest(s):
        return pltpu.make_async_remote_copy(
            src_ref=send_rest.at[0], dst_ref=recv_rest.at[s],
            send_sem=send_rest_sem.at[s], recv_sem=recv_rest_sem.at[s],
            device_id=(my_dp, s), device_id_type=MESH,
        )

    def chip_of(j):
        k = j
        if chips & (chips - 1) == 0:
            return flip_bits(q0, k, chips)
        return (q0 + k) % chips

    def source_of(j):
        if chips & (chips - 1) == 0:
            return chip_of(j)
        k = j
        return (q0 + chips - k) % chips

    def prepare_pair(q):
        prepare(2 * q + c0)
        prepare(2 * q + 1 - c0)

    def send_pair(q):
        for p in range(PARTS):
            for c in (c0, 1 - c0):
                outgoing(2 * q + c, p).start()
                if p == 0:
                    outgoing_rest(2 * q + c).start()

    greeted = everyone - 1
    grad_load.wait()
    load.start()
    if slices == 1:
        prepare_pair(chip_of(jnp.int32(1)))
        pl.semaphore_wait(barrier, greeted)

        def step(j, x):
            prepare_pair(chip_of((j + 1) % chips))
            send_pair(chip_of(j))
            return x
    else:
        def fill(e, x):
            prepare(e)
            return x

        lax.fori_loop(0, experts, fill, 0)
        pl.semaphore_wait(barrier, greeted)

        def step(j, x):
            send_pair(chip_of(j))
            return x

    lax.fori_loop(1, chips, step, 0)
    for p in range(PARTS):
        outgoing(partner, p).start()
    outgoing_rest(partner).start()

    recv[me] = send[own]
    recv_rest[me] = send_rest[own]
    row_peak = jnp.max(jnp.abs(grad_ref[...]).astype(jnp.float32), axis=1, keepdims=True)
    grad_peak = jnp.max(jnp.where(mask_t.T > 0.5, row_peak, 0.0), axis=0, keepdims=True)

    back = 1.0 / pick(scale_in, own)
    own_hidden = pick(scale_hidden, own)
    load.wait()

    def times_weight(block, columns):
        return lax.dot_general(
            block, weight[:, columns], (((1,), (1,)), ((), ())), preferred_element_type=jnp.float32
        )

    def multiply(block):
        return finish(times_weight(block, slice(None)))

    def finish(product):
        hidden = product * back
        scaled = jnp.clip(hidden * own_hidden, -1.0, 1.0)
        return scaled, jnp.max(jnp.max(jnp.abs(hidden), axis=0, keepdims=True), axis=1, keepdims=True)

    def pair_rows(q):
        return recv[pl.ds(2 * q, 2)].reshape(2 * main, recv.shape[2])

    def put_pair(q, scaled):
        for c in range(2):
            held[2 * q + c] = scaled[c * main:(c + 1) * main].astype(jnp.bfloat16)

    def take_own():
        for p in range(PARTS):
            incoming(partner, p).wait_recv()
        scaled, peak = multiply(pair_rows(q0))
        put_pair(q0, scaled)
        return peak

    def take(j, peak):
        q = source_of(j)
        for p in range(PARTS):
            incoming(2 * q, p).wait_recv()
            incoming(2 * q + 1, p).wait_recv()
        scaled, peak_here = multiply(pair_rows(q))
        put_pair(q, scaled)
        return jnp.maximum(peak, peak_here)

    peak = lax.fori_loop(1, chips - 1, take, take_own())

    def take_rest(j, x):
        incoming_rest((me + j) % n_exp).wait_recv()
        return x

    lax.fori_loop(1, n_exp, take_rest, 0)
    rest = capacity - main
    for s in range(n_exp):
        rest_rows[s * rest:(s + 1) * rest, :] = recv_rest[s].astype(jnp.float32)
    last = source_of(jnp.int32(chips - 1))
    product = None
    for p in range(PARTS):
        incoming(2 * last, p).wait_recv()
        incoming(2 * last + 1, p).wait_recv()
        columns = slice(p * span, (p + 1) * span)
        pair = recv[pl.ds(2 * last, 2), :, columns].reshape(2 * main, span)
        block = jnp.concatenate([pair, rest_rows[:, columns].astype(jnp.bfloat16)], axis=0)
        piece = times_weight(block, columns)
        product = piece if product is None else product + piece
    scaled, peak_here = finish(product)
    peak = jnp.maximum(peak, peak_here)

    at = lax.broadcasted_iota(jnp.int32, (1, LANES), 1)
    hidden_peak = jnp.where(at == own, peak, 0.0)
    part = lax.broadcasted_iota(jnp.int32, (8, LANES), 0)
    mine[...] = jnp.where(part == 0, grad_peak, jnp.where(part == 1, hidden_peak, 0.0))

    def peak_copy(peer, slot, j):
        return pltpu.make_async_remote_copy(
            src_ref=mine, dst_ref=peaks_in.at[slot],
            send_sem=peak_send_sem.at[j], recv_sem=peak_recv_sem.at[slot],
            device_id=(peer // n_exp, peer % n_exp), device_id_type=MESH,
        )

    def peak_start(j, x):
        peak_copy((here + j) % everyone, here, j).start()
        return x

    def peak_fold(j, best):
        peer = (here + j) % everyone
        peak_copy(peer, peer, j).wait_recv()
        return jnp.maximum(best, peaks_in[peer])

    def peak_finish(j, x):
        peak_copy((here + j) % everyone, here, j).wait_send()
        return x

    lax.fori_loop(1, everyone, peak_start, 0)
    put_pair(last, scaled)
    for s in range(n_exp):
        at_row = 2 * main + s * rest
        base = s * capacity
        out_ref[base:base + main, :] = held[s]
        out_ref[base + main:base + capacity, :] = scaled[at_row:at_row + rest].astype(jnp.bfloat16)
    best = lax.fori_loop(1, everyone, peak_fold, mine[...])
    lax.fori_loop(1, everyone, peak_finish, 0)

    best_ref[...] = best

    def drain(j, x):
        for p in range(PARTS):
            outgoing((me + j) % n_exp, p).wait_send()
        outgoing_rest((me + j) % n_exp).wait_send()
        return x

    lax.fori_loop(1, n_exp, drain, 0)


def finish_kernel(hist_g_ref, hist_h_ref, best_ref, out_ref, new_g_ref, new_h_ref, final_ref):
    final_ref[...] = out_ref[...]
    keep = hist_g_ref.shape[0] - 1
    experts = hist_g_ref.shape[1]
    new_g_ref[0:keep, :] = hist_g_ref[1:keep + 1, :]
    new_g_ref[keep:keep + 1, :] = best_ref[0:1, 0:experts]
    new_h_ref[0:keep, :] = hist_h_ref[1:keep + 1, :]
    new_h_ref[keep:keep + 1, :] = best_ref[1:2, 0:experts]


def per_device(grad_out, expert_ids, down_weight, history_grad, history_hidden):
    tokens, width = grad_out.shape
    experts = history_grad.shape[1]
    n_dp, n_exp = lax.axis_size("dp"), lax.axis_size("expert")
    capacity = tokens * 9 // 32
    main = (capacity - 1) // 16 * 16
    rest = capacity - main
    units = down_weight.shape[1]
    vmem = pl.BlockSpec(memory_space=pltpu.VMEM)
    dma = pltpu.SemaphoreType.DMA
    out, best = pl.pallas_call(
        functools.partial(kernel, n_dp, n_exp, experts, capacity),
        out_shape=(
            jax.ShapeDtypeStruct((n_exp * capacity, units), jnp.bfloat16),
            jax.ShapeDtypeStruct((8, LANES), jnp.float32),
        ),
        in_specs=[pl.BlockSpec(memory_space=pl.ANY), vmem, vmem, vmem, pl.BlockSpec(memory_space=pl.ANY)],
        out_specs=(vmem, vmem),
        scratch_shapes=[
            pltpu.VMEM((tokens, width), jnp.bfloat16),
            pltpu.VMEM((n_exp, main, units), jnp.bfloat16),
            pltpu.VMEM((units, width), jnp.bfloat16),
            pltpu.VMEM((experts, main, width), jnp.bfloat16),
            pltpu.VMEM((experts, rest, width), jnp.bfloat16),
            pltpu.VMEM((n_exp, main, width), jnp.bfloat16),
            pltpu.VMEM((n_exp, rest, width), jnp.bfloat16),
            pltpu.VMEM((n_exp * rest, width), jnp.float32),
            pltpu.VMEM((LANES, tokens), jnp.float32),
            pltpu.VMEM((8, LANES), jnp.float32),
            pltpu.VMEM((n_dp * n_exp, 8, LANES), jnp.float32),
            dma, dma, dma((PARTS, n_exp)), dma((PARTS, n_exp)), dma((n_exp,)), dma((n_exp,)),
            dma((n_dp * n_exp,)), dma((n_dp * n_exp,)),
        ],
        compiler_params=pltpu.CompilerParams(
            collective_id=0, has_side_effects=True, vmem_limit_bytes=60 * 1024 * 1024
        ),
    )(grad_out, expert_ids.T, history_grad, history_hidden, down_weight)
    new_g, new_h, out = pl.pallas_call(
        finish_kernel,
        out_shape=(
            jax.ShapeDtypeStruct(history_grad.shape, jnp.float32),
            jax.ShapeDtypeStruct(history_hidden.shape, jnp.float32),
            jax.ShapeDtypeStruct(out.shape, out.dtype),
        ),
        in_specs=[vmem, vmem, vmem, vmem],
        out_specs=(vmem, vmem, vmem),
    )(history_grad, history_hidden, best, out)
    return out.reshape(1, 1, n_exp * capacity, units), new_g, new_h


def solution(mesh):
    in_specs = (
        P(("dp", "expert"), None),
        P(("dp", "expert"), None),
        P("expert", None, None),
        P(),
        P(),
    )
    out_specs = (P("dp", "expert", None, None), P(), P())
    return jax.shard_map(
        per_device, mesh=mesh, in_specs=in_specs, out_specs=out_specs, check_vma=False
    )
```

profile of v0, /device:TPU:0, one launch (start us, length us, event | category | flops | bytes accessed | tf_op | source)
XLA Modules:
  0.0 58.9 jit_solution(12801691303779879993)
XLA Ops:
  0.6 56.3 %shard_map.76 = (bf16[288,1024]{1,0:T(8,128)(2,1)}, f32[8,128]{1,0:T(8,128)}) custom-call(bf16[128,3072]{1,0:T(8,128)(2,1)} %grad_hbm.1, s32[2,128]{1,0:T(2,128)} %bitcast.2, f32[8,8]{1,0:T(8,128)} %hist_g_ref.3, f32[8,8]{1,0:T(8,128)} %hist_h_ref.3, bf16[1,1024,3072]{2,1,0:T(8,128)(2,1)} %weight_hbm.1), custom_call_target="tpu_custom_call" | custom-call | tf_op jit(solution)/shard_map/pallas_call | solution.py:298
  57.0 2.0 %shard_map.77 = (f32[8,8]{1,0:T(8,128)}, f32[8,8]{1,0:T(8,128)}, bf16[288,1024]{1,0:T(8,128)(2,1)}) custom-call(f32[8,8]{1,0:T(8,128)} %hist_g_ref.3, f32[8,8]{1,0:T(8,128)} %hist_h_ref.3, f32[8,128]{1,0:T(8,128)} %get-tuple-element.8.best_ref, bf16[288,1024]{1,0:T(8,128)(2,1)} %get-tuple-element.9.out_ref), custom_call_target="tpu_custom_call" | custom-call | tf_op jit(solution)/shard_map/pallas_call | solution.py:325
where the time goes:
time: 59.1 us; the launch traced here: 58.9 us
  Pallas kernels  58.3 us (99%)
  between operations  0.64 us (1%)
    pallas_call x1, Pallas kernels, per_device(): pl.pallas_call(functools.partial(kernel, n_dp, n_exp, experts, capacity),...  56.3 us
    pallas_call x1, Pallas kernels, per_device(): pl.pallas_call(finish_kernel, out_shape=(jax.ShapeDtypeStruct(history_gra...  1.96 us

commit v1 on v0

--- a/solution.py
+++ b/solution.py
@@ -10,6 +10,7 @@
 MESH = pl.DeviceIdType.MESH
 PARTS = 4
 LANES = 128
+RELAY_PARTS = 6
 
 
 def flip_bits(q, k, count):
@@ -285,7 +286,7 @@
     new_h_ref[keep:keep + 1, :] = best_ref[1:2, 0:experts]
 
 
-def per_device(grad_out, expert_ids, down_weight, history_grad, history_hidden):
+def by_blocks(grad_out, expert_ids, down_weight, history_grad, history_hidden):
     tokens, width = grad_out.shape
     experts = history_grad.shape[1]
     n_dp, n_exp = lax.axis_size("dp"), lax.axis_size("expert")
@@ -335,6 +336,446 @@
     return out.reshape(1, 1, n_exp * capacity, units), new_g, new_h
 
 
+def relay_kernel(
+    n_dp, n_exp, experts, capacity, parts,
+    grad_hbm, ids_ref, hist_g_ref, hist_h_ref, weight_hbm,
+    out_ref, best_ref,
+    grad, raw, weight, send, send_rest, far, far_rest, relay, relay_rest, recv, recv_rest,
+    rest_rows, acc, slots, slots_in, onehot, mine, peaks_in,
+    grad_sem, weight_sem, raw_send, raw_recv, slot_send, slot_recv,
+    near_send, near_rest_send, far_send, far_rest_send, near_recv, near_rest_recv,
+    relay_send, relay_rest_send, relay_recv, relay_rest_recv, peak_send, peak_recv,
+):
+    tokens, width = grad.shape
+    main = send.shape[1]
+    rest = capacity - main
+    half = n_exp // 2
+    deep = n_exp // 4
+    span = width // parts
+    last = parts - 1
+    my_dp, me = lax.axis_index("dp"), lax.axis_index("expert")
+    q0, c0 = me // 2, me % 2
+    side = q0 // deep
+    base, far_base = side * half, (1 - side) * half
+    my_i, my_k = me - base, q0 - side * deep
+    inner = q0 == deep - 1 + side
+    relay_dev = 2 * (deep - side) + c0
+    everyone = n_dp * n_exp
+    here = my_dp * n_exp + me
+
+    grad_load = pltpu.make_async_copy(grad_hbm, grad, grad_sem)
+    grad_load.start()
+    load = pltpu.make_async_copy(weight_hbm.at[0], weight, weight_sem)
+    barrier = pltpu.get_barrier_semaphore()
+
+    def greet(j, x):
+        peer = (here + j) % everyone
+        pl.semaphore_signal(
+            barrier, inc=1, device_id=(peer // n_exp, peer % n_exp), device_id_type=MESH
+        )
+        return x
+
+    lax.fori_loop(1, everyone, greet, 0)
+
+    expert_row = lax.broadcasted_iota(jnp.int32, (LANES, tokens), 0)
+    ids = ids_ref[...]
+    mask_t = jnp.where((ids[0:1, :] == expert_row) | (ids[1:2, :] == expert_row), 1.0, 0.0)
+    row = lax.broadcasted_iota(jnp.int32, (tokens, tokens), 0)
+    col = lax.broadcasted_iota(jnp.int32, (tokens, tokens), 1)
+    earlier = jnp.where(row < col, 1.0, 0.0).astype(jnp.bfloat16)
+    before = jnp.dot(mask_t.astype(jnp.bfloat16), earlier, preferred_element_type=jnp.float32)
+    slots[...] = jnp.where(mask_t > 0.5, before, -1.0)
+    scale_in = 1.0 / jnp.max(hist_g_ref[...], axis=0, keepdims=True)
+    scale_hidden = 1.0 / jnp.max(hist_h_ref[...], axis=0, keepdims=True)
+    which = lax.broadcasted_iota(jnp.int32, (1, experts), 1)
+
+    def pick(values, e):
+        return jnp.sum(jnp.where(which == e, values, 0.0), axis=1, keepdims=True)
+
+    position = lax.broadcasted_iota(jnp.int32, (main, tokens), 0).astype(jnp.float32)
+    rest_row = lax.broadcasted_iota(jnp.int32, (half * rest, tokens), 0)
+    rest_position = (rest_row % rest + main).astype(jnp.float32)
+    rest_group = rest_row // rest
+
+    def spread(at, slot_row, first):
+        spare = jnp.full((half * rest, tokens), -1.0, jnp.float32)
+        for i in range(half):
+            named = slot_row(first + i)
+            onehot[at, i * main:(i + 1) * main, :] = jnp.where(
+                named == position, 1.0, 0.0
+            ).astype(jnp.bfloat16)
+            spare = jnp.where(rest_group == i, named, spare)
+        onehot[at, half * main:half * capacity, :] = jnp.where(
+            spare == rest_position, 1.0, 0.0
+        ).astype(jnp.bfloat16)
+
+    def own_row(e):
+        return slots[pl.ds(e, 1), :]
+
+    group_column = lax.broadcasted_iota(jnp.int32, (half * rest, 1), 0) // rest
+
+    def scales_of(first):
+        scales = [pick(scale_in, first + i) for i in range(half)]
+        spare = jnp.zeros((half * rest, 1), jnp.float32)
+        for i in range(half):
+            spare = jnp.where(group_column == i, scales[i], spare)
+        return scales, spare
+
+    def fill(at, source, scales, put, put_rest):
+        rows = jnp.dot(onehot[at], source, preferred_element_type=jnp.float32)
+        each, spare = scales
+        for i in range(half):
+            put(i, jnp.clip(rows[i * main:(i + 1) * main] * each[i], -1.0, 1.0).astype(jnp.bfloat16))
+        ends = jnp.clip(rows[half * main:half * capacity] * spare, -1.0, 1.0)
+        for i in range(half):
+            put_rest(i, ends[i * rest:(i + 1) * rest].astype(jnp.bfloat16))
+
+    def columns_of(p):
+        if isinstance(p, int):
+            return pl.ds(p * span, span)
+        return pl.ds(pl.multiple_of(p * span, span), span)
+
+    def remote(src, dst, send_sem, recv_sem, d):
+        return pltpu.make_async_remote_copy(
+            src_ref=src, dst_ref=dst, send_sem=send_sem, recv_sem=recv_sem,
+            device_id=(my_dp, d), device_id_type=MESH,
+        )
+
+    def raw_copy(p, k):
+        columns = columns_of(p)
+        return remote(
+            grad.at[:, columns], raw.at[k, :, columns], raw_send.at[p], raw_recv.at[p, k], relay_dev
+        )
+
+    def slot_copy(k):
+        return remote(slots.at[pl.ds(0, experts)], slots_in.at[k], slot_send, slot_recv.at[k], relay_dev)
+
+    def near_copy(p, i, at):
+        columns = columns_of(p)
+        return remote(
+            send.at[i, :, columns], recv.at[at, :, columns],
+            near_send.at[p, i], near_recv.at[p, at], base + i,
+        )
+
+    def near_rest_copy(p, i, at):
+        columns = columns_of(p)
+        return remote(
+            send_rest.at[i, :, columns], recv_rest.at[at, :, columns],
+            near_rest_send.at[p, i], near_rest_recv.at[p, at], base + i,
+        )
+
+    def far_copy(i, at):
+        return remote(
+            far.at[i], recv.at[at, :, columns_of(last)],
+            far_send.at[i], near_recv.at[last, at], far_base + i,
+        )
+
+    def far_rest_copy(i, at):
+        return remote(
+            far_rest.at[i], recv_rest.at[at, :, columns_of(last)],
+            far_rest_send.at[i], near_rest_recv.at[last, at], far_base + i,
+        )
+
+    def relay_copy(p, i, c):
+        columns = columns_of(p)
+        return remote(
+            relay.at[i, :, :, columns], recv.at[pl.ds(half + c * deep, deep), :, columns],
+            relay_send.at[p, i], relay_recv.at[p, c], base + i,
+        )
+
+    def relay_rest_copy(p, i, c):
+        columns = columns_of(p)
+        return remote(
+            relay_rest.at[i, :, :, columns], recv_rest.at[pl.ds(half + c * deep, deep), :, columns],
+            relay_rest_send.at[p, i], relay_rest_recv.at[p, c], base + i,
+        )
+
+    spread(0, own_row, base)
+    spread(1, own_row, far_base)
+    near_scales = scales_of(base)
+    grad_load.wait()
+    load.start()
+    pl.semaphore_wait(barrier, everyone - 1)
+    slot_copy(my_k).start()
+    raw_copy(0, my_k).start()
+
+    @pl.when(inner)
+    def _():
+        def more(p, x):
+            raw_copy(p, my_k).start()
+            return x
+
+        lax.fori_loop(1, last, more, 0)
+
+    def direct(p, x):
+        columns = columns_of(p)
+
+        def put(i, block):
+            send[i, :, columns] = block
+
+        def put_rest(i, block):
+            send_rest[i, :, columns] = block
+
+        fill(0, grad[:, columns], near_scales, put, put_rest)
+        for j in range(1, half):
+            i = (my_i + j) % half
+            near_copy(p, i, my_i).start()
+            near_rest_copy(p, i, my_i).start()
+
+        @pl.when(jnp.logical_not(inner) & (p + 1 < last))
+        def _():
+            raw_copy(p + 1, my_k).start()
+
+        return x
+
+    lax.fori_loop(0, parts, direct, 0)
+
+    def put_far(i, block):
+        far[i] = block
+
+    def put_far_rest(i, block):
+        far_rest[i] = block
+
+    fill(1, grad[:, columns_of(last)], scales_of(far_base), put_far, put_far_rest)
+    far_at = half + c0 * deep + my_k
+    for i in range(half):
+        far_copy(i, far_at).start()
+        far_rest_copy(i, far_at).start()
+
+    recv[my_i] = send[my_i]
+    recv_rest[my_i] = send_rest[my_i]
+    row_peak = jnp.max(jnp.abs(grad[...]).astype(jnp.float32), axis=1, keepdims=True)
+    grad_peak = jnp.max(jnp.where(mask_t.T > 0.5, row_peak, 0.0), axis=0, keepdims=True)
+    back = 1.0 / pick(scale_in, me)
+    own_hidden = pick(scale_hidden, me)
+    acc[...] = jnp.zeros_like(acc)
+
+    @pl.when(inner)
+    def _():
+        for k in range(deep):
+            slot_copy(k).wait_recv()
+            spread(2 + k, lambda e: slots_in[k, pl.ds(e, 1), :], base)
+
+    load.wait()
+
+    def product_of(p):
+        columns = columns_of(p)
+        for s in range(n_exp):
+            rest_rows[s * rest:(s + 1) * rest, :] = recv_rest[s, :, columns].astype(jnp.float32)
+        block = jnp.concatenate(
+            [recv[:, :, columns].reshape(n_exp * main, span), rest_rows[...].astype(jnp.bfloat16)], axis=0
+        )
+        return lax.dot_general(
+            block, weight[:, columns], (((1,), (1,)), ((), ())), preferred_element_type=jnp.float32
+        )
+
+    def take(p, x):
+        columns = columns_of(p)
+
+        @pl.when(inner)
+        def _():
+            for k in range(deep):
+                raw_copy(p, k).wait_recv()
+
+                def put(i, block):
+                    relay[i, k, :, columns] = block
+
+                def put_rest(i, block):
+                    relay_rest[i, k, :, columns] = block
+
+                fill(2 + k, raw[k, :, columns], near_scales, put, put_rest)
+            for j in range(1, half):
+                i = (my_i + j) % half
+                relay_copy(p, i, c0).start()
+                relay_rest_copy(p, i, c0).start()
+            for k in range(deep):
+                recv[half + c0 * deep + k, :, columns] = relay[my_i, k, :, columns]
+                recv_rest[half + c0 * deep + k, :, columns] = relay_rest[my_i, k, :, columns]
+
+        for j in range(1, half):
+            i = (my_i + j) % half
+            near_copy(p, i, i).wait_recv()
+            near_rest_copy(p, i, i).wait_recv()
+        relay_copy(p, 0, 1 - c0).wait_recv()
+        relay_rest_copy(p, 0, 1 - c0).wait_recv()
+
+        @pl.when(jnp.logical_not(inner))
+        def _():
+            relay_copy(p, 0, c0).wait_recv()
+            relay_rest_copy(p, 0, c0).wait_recv()
+
+        acc[...] = acc[...] + product_of(p)
+        return x
+
+    lax.fori_loop(0, last, take, 0)
+
+    for j in range(1, half):
+        i = (my_i + j) % half
+        near_copy(last, i, i).wait_recv()
+        near_rest_copy(last, i, i).wait_recv()
+    for at in range(half, n_exp):
+        far_copy(0, at).wait_recv()
+        far_rest_copy(0, at).wait_recv()
+    acc[...] = acc[...] + product_of(last)
+    hidden = acc[...] * back
+    peak = jnp.max(jnp.max(jnp.abs(hidden), axis=0, keepdims=True), axis=1, keepdims=True)
+    lane = lax.broadcasted_iota(jnp.int32, (1, LANES), 1)
+    mine[...] = jnp.where(lane < experts, grad_peak, jnp.where(lane == experts + me, peak, 0.0))
+
+    def peak_copy(peer, slot, j):
+        return pltpu.make_async_remote_copy(
+            src_ref=mine, dst_ref=peaks_in.at[slot],
+            send_sem=peak_send.at[j], recv_sem=peak_recv.at[slot],
+            device_id=(peer // n_exp, peer % n_exp), device_id_type=MESH,
+        )
+
+    def peak_start(j, x):
+        peak_copy((here + j) % everyone, here, j).start()
+        return x
+
+    lax.fori_loop(1, everyone, peak_start, 0)
+
+    scaled = jnp.clip(acc[...] * back * own_hidden, -1.0, 1.0)
+    for at in range(n_exp):
+        if at < half:
+            block, first = side, at * capacity
+        else:
+            block, first = 1 - side, ((at - half) % deep * 2 + (at - half) // deep) * capacity
+        out_ref[block, first:first + main, :] = scaled[at * main:(at + 1) * main].astype(jnp.bfloat16)
+        tail = n_exp * main + at * rest
+        out_ref[block, first + main:first + capacity, :] = scaled[tail:tail + rest].astype(jnp.bfloat16)
+
+    def peak_fold(j, best):
+        peer = (here + j) % everyone
+        peak_copy(peer, peer, j).wait_recv()
+        return jnp.maximum(best, peaks_in[peer])
+
+    best_ref[...] = lax.fori_loop(1, everyone, peak_fold, mine[...])
+
+    def peak_finish(j, x):
+        peak_copy((here + j) % everyone, here, j).wait_send()
+        return x
+
+    lax.fori_loop(1, everyone, peak_finish, 0)
+    slot_copy(my_k).wait_send()
+
+    def drain(p, x):
+        for j in range(1, half):
+            i = (my_i + j) % half
+            near_copy(p, i, my_i).wait_send()
+            near_rest_copy(p, i, my_i).wait_send()
+
+        @pl.when(p < last)
+        def _():
+            raw_copy(p, my_k).wait_send()
+
+        @pl.when(inner & (p < last))
+        def _():
+            for j in range(1, half):
+                i = (my_i + j) % half
+                relay_copy(p, i, c0).wait_send()
+                relay_rest_copy(p, i, c0).wait_send()
+
+        return x
+
+    lax.fori_loop(0, parts, drain, 0)
+    for i in range(half):
+        far_copy(i, far_at).wait_send()
+        far_rest_copy(i, far_at).wait_send()
+
+
+def relay_finish(hist_g_ref, hist_h_ref, best_ref, out_ref, new_g_ref, new_h_ref, final_ref):
+    final_ref[...] = out_ref[...]
+    keep = hist_g_ref.shape[0] - 1
+    experts = hist_g_ref.shape[1]
+    new_g_ref[0:keep, :] = hist_g_ref[1:keep + 1, :]
+    new_g_ref[keep:keep + 1, :] = best_ref[0:1, 0:experts]
+    new_h_ref[0:keep, :] = hist_h_ref[1:keep + 1, :]
+    new_h_ref[keep:keep + 1, :] = best_ref[0:1, experts:2 * experts]
+
+
+def by_relay(grad_out, expert_ids, down_weight, history_grad, history_hidden):
+    tokens, width = grad_out.shape
+    experts = history_grad.shape[1]
+    n_dp, n_exp = lax.axis_size("dp"), lax.axis_size("expert")
+    capacity = tokens * 9 // 32
+    main = (capacity - 1) // 16 * 16
+    rest = capacity - main
+    units = down_weight.shape[1]
+    half, deep = n_exp // 2, n_exp // 4
+    parts = RELAY_PARTS
+    span = width // parts
+    everyone = n_dp * n_exp
+    vmem = pl.BlockSpec(memory_space=pltpu.VMEM)
+    dma = pltpu.SemaphoreType.DMA
+    bf16, f32 = jnp.bfloat16, jnp.float32
+    out, best = pl.pallas_call(
+        functools.partial(relay_kernel, n_dp, n_exp, experts, capacity, parts),
+        out_shape=(
+            jax.ShapeDtypeStruct((2, half * capacity, units), bf16),
+            jax.ShapeDtypeStruct((1, LANES), f32),
+        ),
+        in_specs=[pl.BlockSpec(memory_space=pl.ANY), vmem, vmem, vmem, pl.BlockSpec(memory_space=pl.ANY)],
+        out_specs=(vmem, vmem),
+        scratch_shapes=[
+            pltpu.VMEM((tokens, width), bf16),
+            pltpu.VMEM((deep, tokens, width), bf16),
+            pltpu.VMEM((units, width), bf16),
+            pltpu.VMEM((half, main, width), bf16),
+            pltpu.VMEM((half, rest, width), bf16),
+            pltpu.VMEM((half, main, span), bf16),
+            pltpu.VMEM((half, rest, span), bf16),
+            pltpu.VMEM((half, deep, main, width), bf16),
+            pltpu.VMEM((half, deep, rest, width), bf16),
+            pltpu.VMEM((n_exp, main, width), bf16),
+            pltpu.VMEM((n_exp, rest, width), bf16),
+            pltpu.VMEM((n_exp * rest, span), f32),
+            pltpu.VMEM((n_exp * capacity, units), f32),
+            pltpu.VMEM((LANES, tokens), f32),
+            pltpu.VMEM((deep, experts, tokens), f32),
+            pltpu.VMEM((2 + deep, half * capacity, tokens), bf16),
+            pltpu.VMEM((1, LANES), f32),
+            pltpu.VMEM((everyone, 1, LANES), f32),
+            dma, dma, dma((parts,)), dma((parts, deep)), dma, dma((deep,)),
+            dma((parts, half)), dma((parts, half)), dma((half,)), dma((half,)),
+            dma((parts, n_exp)), dma((parts, n_exp)),
+            dma((parts, half)), dma((parts, half)), dma((parts, 2)), dma((parts, 2)),
+            dma((everyone,)), dma((everyone,)),
+        ],
+        compiler_params=pltpu.CompilerParams(
+            collective_id=1, has_side_effects=True, vmem_limit_bytes=60 * 1024 * 1024
+        ),
+    )(grad_out, expert_ids.T, history_grad, history_hidden, down_weight)
+    new_g, new_h, out = pl.pallas_call(
+        relay_finish,
+        out_shape=(
+            jax.ShapeDtypeStruct(history_grad.shape, f32),
+            jax.ShapeDtypeStruct(history_hidden.shape, f32),
+            jax.ShapeDtypeStruct(out.shape, out.dtype),
+        ),
+        in_specs=[vmem, vmem, vmem, vmem],
+        out_specs=(vmem, vmem, vmem),
+    )(history_grad, history_hidden, best, out)
+    return out.reshape(1, 1, n_exp * capacity, units), new_g, new_h
+
+
+def fits_relay(tokens, width, experts, n_exp):
+    capacity = tokens * 9 // 32
+    return (
+        experts == n_exp and n_exp % 4 == 0 and experts % 8 == 0 and 2 * experts <= LANES
+        and tokens % LANES == 0 and width % (RELAY_PARTS * LANES) == 0
+        and (n_exp // 2 * capacity) % 16 == 0 and (n_exp // 2 * (capacity % 16)) % 16 == 0
+        and 0 < capacity % 16
+    )
+
+
+def per_device(*arguments):
+    (tokens, width), experts = arguments[0].shape, arguments[3].shape[1]
+    if fits_relay(tokens, width, experts, lax.axis_size("expert")):
+        return by_relay(*arguments)
+    return by_blocks(*arguments)
+
+
 def solution(mesh):
     in_specs = (
         P(("dp", "expert"), None),

time: 59.1 us -> 59.3 us (level)
  no operation moved by 1% of the time
where the time goes in v1:
time: 59.3 us; the launch traced here: 59 us
  Pallas kernels  58.4 us (98%)
  between operations  0.64 us (1%)
    pallas_call x1, Pallas kernels, by_relay(): pl.pallas_call(functools.partial(relay_kernel, n_dp, n_exp, experts, capa...  56.4 us
    pallas_call x1, Pallas kernels, by_relay(): pl.pallas_call(relay_finish, out_shape=(jax.ShapeDtypeStruct(history_grad...  1.99 us

profile of v1, /device:TPU:0, one launch (start us, length us, event | category | flops | bytes accessed | tf_op | source)
XLA Modules:
  0.0 59.0 jit_solution(1301173715790312574)
XLA Ops:
  0.6 56.4 %shard_map.76 = (bf16[2,144,1024]{2,1,0:T(8,128)(2,1)}, f32[1,128]{1,0:T(1,128)}) custom-call(bf16[128,3072]{1,0:T(8,128)(2,1)} %grad_hbm.1, s32[2,128]{1,0:T(2,128)} %bitcast.2, f32[8,8]{1,0:T(8,128)} %hist_g_ref.3, f32[8,8]{1,0:T(8,128)} %hist_h_ref.3, bf16[1,1024,3072]{2,1,0:T(8,128)(2,1)} %weight_hbm.1), custom_call_target="tpu_custom_call" | custom-call | tf_op jit(solution)/shard_map/pallas_call | solution.py:712
  57.1 2.0 %shard_map.77 = (f32[8,8]{1,0:T(8,128)}, f32[8,8]{1,0:T(8,128)}, bf16[2,144,1024]{2,1,0:T(8,128)(2,1)}) custom-call(f32[8,8]{1,0:T(8,128)} %hist_g_ref.3, f32[8,8]{1,0:T(8,128)} %hist_h_ref.3, f32[1,128]{1,0:T(1,128)} %get-tuple-element.8.best_ref, bf16[2,144,1024]{2,1,0:T(8,128)(2,1)} %get-tuple-element.9.out_ref), custom_call_target="tpu_custom_call" | custom-call | tf_op jit(solution)/shard_map/pallas_call | solution.py:749

commit v2 on v1

--- a/solution.py
+++ b/solution.py
@@ -10,7 +10,8 @@
 MESH = pl.DeviceIdType.MESH
 PARTS = 4
 LANES = 128
-RELAY_PARTS = 6
+RELAY_CHUNKS = 12
+RELAY_DIRECT = 3
 
 
 def flip_bits(q, k, count):
@@ -337,52 +338,72 @@
 
 
 def relay_kernel(
-    n_dp, n_exp, experts, capacity, parts,
-    grad_hbm, ids_ref, hist_g_ref, hist_h_ref, weight_hbm,
+    n_dp, n_exp, experts, capacity, chunks,
+    grad_hbm, ids_hbm, hist_g_hbm, hist_h_hbm, weight_hbm,
     out_ref, best_ref,
-    grad, raw, weight, send, send_rest, far, far_rest, relay, relay_rest, recv, recv_rest,
+    grad, ids_ref, hist_g_ref, hist_h_ref, raw, weight,
+    send, send_rest, far, far_rest, relay, relay_rest, recv, recv_rest,
     rest_rows, acc, slots, slots_in, onehot, mine, peaks_in,
-    grad_sem, weight_sem, raw_send, raw_recv, slot_send, slot_recv,
-    near_send, near_rest_send, far_send, far_rest_send, near_recv, near_rest_recv,
-    relay_send, relay_rest_send, relay_recv, relay_rest_recv, peak_send, peak_recv,
+    load_sem, known, slot_send, slot_recv, raw_send, raw_recv,
+    near_send, near_rest_send, far_send, far_rest_send, relay_send, relay_rest_send,
+    main_recv, rest_recv, peak_send, peak_recv,
 ):
     tokens, width = grad.shape
     main = send.shape[1]
     rest = capacity - main
-    half = n_exp // 2
-    deep = n_exp // 4
-    span = width // parts
-    last = parts - 1
+    half, deep = n_exp // 2, n_exp // 4
+    relayed = raw.shape[2]
+    span = width // chunks
+    hops = relayed // span
     my_dp, me = lax.axis_index("dp"), lax.axis_index("expert")
     q0, c0 = me // 2, me % 2
     side = q0 // deep
     base, far_base = side * half, (1 - side) * half
     my_i, my_k = me - base, q0 - side * deep
     inner = q0 == deep - 1 + side
-    relay_dev = 2 * (deep - side) + c0
+    outer = jnp.logical_not(inner)
+    partner = q0 * 2 + 1 - c0
+    across = 2 * (deep - side) + c0
+    behind = 2 * (deep - 1 + side + jnp.where(inner, 2 * side - 1, 0)) + c0
     everyone = n_dp * n_exp
     here = my_dp * n_exp + me
 
-    grad_load = pltpu.make_async_copy(grad_hbm, grad, grad_sem)
+    def loading(src, dst, at):
+        return pltpu.make_async_copy(src, dst, load_sem.at[at])
+
+    small = (
+        loading(ids_hbm, ids_ref, 0), loading(hist_g_hbm, hist_g_ref, 1), loading(hist_h_hbm, hist_h_ref, 2)
+    )
+    grad_load = loading(grad_hbm, grad, 3)
+    load = loading(weight_hbm.at[0], weight, 4)
+    for copy in small:
+        copy.start()
     grad_load.start()
-    load = pltpu.make_async_copy(weight_hbm.at[0], weight, weight_sem)
+
+    def tell(semaphore, d, dp=None):
+        pl.semaphore_signal(
+            semaphore, inc=1, device_id=(my_dp if dp is None else dp, d), device_id_type=MESH
+        )
+
     barrier = pltpu.get_barrier_semaphore()
 
-    def greet(j, x):
-        peer = (here + j) % everyone
-        pl.semaphore_signal(
-            barrier, inc=1, device_id=(peer // n_exp, peer % n_exp), device_id_type=MESH
-        )
-        return x
-
-    lax.fori_loop(1, everyone, greet, 0)
+    @pl.when(inner)
+    def _():
+        tell(barrier, across)
+        tell(barrier, behind)
+
+    tell(barrier, partner)
+    for d in range(1, n_dp):
+        tell(barrier, me, (my_dp + d) % n_dp)
 
     expert_row = lax.broadcasted_iota(jnp.int32, (LANES, tokens), 0)
-    ids = ids_ref[...]
-    mask_t = jnp.where((ids[0:1, :] == expert_row) | (ids[1:2, :] == expert_row), 1.0, 0.0)
     row = lax.broadcasted_iota(jnp.int32, (tokens, tokens), 0)
     col = lax.broadcasted_iota(jnp.int32, (tokens, tokens), 1)
     earlier = jnp.where(row < col, 1.0, 0.0).astype(jnp.bfloat16)
+    for copy in small:
+        copy.wait()
+    ids = ids_ref[...]
+    mask_t = jnp.where((ids[0:1, :] == expert_row) | (ids[1:2, :] == expert_row), 1.0, 0.0)
     before = jnp.dot(mask_t.astype(jnp.bfloat16), earlier, preferred_element_type=jnp.float32)
     slots[...] = jnp.where(mask_t > 0.5, before, -1.0)
     scale_in = 1.0 / jnp.max(hist_g_ref[...], axis=0, keepdims=True)
@@ -431,8 +452,6 @@
             put_rest(i, ends[i * rest:(i + 1) * rest].astype(jnp.bfloat16))
 
     def columns_of(p):
-        if isinstance(p, int):
-            return pl.ds(p * span, span)
         return pl.ds(pl.multiple_of(p * span, span), span)
 
     def remote(src, dst, send_sem, recv_sem, d):
@@ -441,71 +460,90 @@
             device_id=(my_dp, d), device_id_type=MESH,
         )
 
-    def raw_copy(p, k):
+    def sent(ref, send_sem):
+        remote(ref, ref, send_sem, send_sem, partner).wait_send()
+
+    def came(ref, recv_sem):
+        remote(ref, ref, recv_sem, recv_sem, partner).wait_recv()
+
+    def send_raw(p):
         columns = columns_of(p)
-        return remote(
-            grad.at[:, columns], raw.at[k, :, columns], raw_send.at[p], raw_recv.at[p, k], relay_dev
-        )
-
-    def slot_copy(k):
-        return remote(slots.at[pl.ds(0, experts)], slots_in.at[k], slot_send, slot_recv.at[k], relay_dev)
-
-    def near_copy(p, i, at):
+        remote(
+            grad.at[:, columns], raw.at[my_k, :, columns], raw_send, raw_recv.at[p], across
+        ).start()
+
+    def send_slots():
+        remote(slots.at[pl.ds(0, experts)], slots_in.at[my_k], slot_send, slot_recv, across).start()
+
+    def send_near(p):
         columns = columns_of(p)
-        return remote(
-            send.at[i, :, columns], recv.at[at, :, columns],
-            near_send.at[p, i], near_recv.at[p, at], base + i,
-        )
-
-    def near_rest_copy(p, i, at):
+        for j in range(1, half):
+            i = (my_i + j) % half
+            remote(
+                send.at[i, :, columns], recv.at[my_i, :, columns], near_send, main_recv.at[p], base + i
+            ).start()
+            remote(
+                send_rest.at[i, :, columns], recv_rest.at[my_i, :, columns],
+                near_rest_send, rest_recv.at[p], base + i,
+            ).start()
+
+    def send_far(p):
+        columns, at = columns_of(p), half + c0 * deep + my_k
+        for j in range(half):
+            i = (my_i + j) % half
+            remote(
+                far.at[i, :, columns_of(p - hops)], recv.at[at, :, columns],
+                far_send, main_recv.at[p], far_base + i,
+            ).start()
+            remote(
+                far_rest.at[i, :, columns_of(p - hops)], recv_rest.at[at, :, columns],
+                far_rest_send, rest_recv.at[p], far_base + i,
+            ).start()
+
+    def send_relay(p):
+        columns, at = columns_of(p), pl.ds(half + c0 * deep, deep)
+        for j in range(1, half):
+            i = (my_i + j) % half
+            remote(
+                relay.at[i, :, :, columns], recv.at[at, :, columns],
+                relay_send, main_recv.at[p], base + i,
+            ).start()
+            remote(
+                relay_rest.at[i, :, :, columns], recv_rest.at[at, :, columns],
+                relay_rest_send, rest_recv.at[p], base + i,
+            ).start()
+
+    def wait_chunk(p, senders):
         columns = columns_of(p)
-        return remote(
-            send_rest.at[i, :, columns], recv_rest.at[at, :, columns],
-            near_rest_send.at[p, i], near_rest_recv.at[p, at], base + i,
-        )
-
-    def far_copy(i, at):
-        return remote(
-            far.at[i], recv.at[at, :, columns_of(last)],
-            far_send.at[i], near_recv.at[last, at], far_base + i,
-        )
-
-    def far_rest_copy(i, at):
-        return remote(
-            far_rest.at[i], recv_rest.at[at, :, columns_of(last)],
-            far_rest_send.at[i], near_rest_recv.at[last, at], far_base + i,
-        )
-
-    def relay_copy(p, i, c):
-        columns = columns_of(p)
-        return remote(
-            relay.at[i, :, :, columns], recv.at[pl.ds(half + c * deep, deep), :, columns],
-            relay_send.at[p, i], relay_recv.at[p, c], base + i,
-        )
-
-    def relay_rest_copy(p, i, c):
-        columns = columns_of(p)
-        return remote(
-            relay_rest.at[i, :, :, columns], recv_rest.at[pl.ds(half + c * deep, deep), :, columns],
-            relay_rest_send.at[p, i], relay_rest_recv.at[p, c], base + i,
-        )
+        came(recv.at[pl.ds(0, senders), :, columns], main_recv.at[p])
+        came(recv_rest.at[pl.ds(0, senders), :, columns], rest_recv.at[p])
 
     spread(0, own_row, base)
     spread(1, own_row, far_base)
     near_scales = scales_of(base)
     grad_load.wait()
     load.start()
-    pl.semaphore_wait(barrier, everyone - 1)
-    slot_copy(my_k).start()
-    raw_copy(0, my_k).start()
+    pl.semaphore_wait(barrier, n_dp + 1)
+    tell(known.at[0], partner)
 
     @pl.when(inner)
     def _():
+        tell(known.at[0], across)
+        send_slots()
+
         def more(p, x):
-            raw_copy(p, my_k).start()
+            send_raw(p)
             return x
 
-        lax.fori_loop(1, last, more, 0)
+        lax.fori_loop(0, hops, more, 0)
+        pl.semaphore_wait(known.at[0], 3)
+        tell(known.at[1], across)
+        tell(known.at[1], behind)
+
+    @pl.when(outer)
+    def _():
+        tell(known.at[0], behind)
+        pl.semaphore_wait(known.at[0], 1)
 
     def direct(p, x):
         columns = columns_of(p)
@@ -517,31 +555,48 @@
             send_rest[i, :, columns] = block
 
         fill(0, grad[:, columns], near_scales, put, put_rest)
-        for j in range(1, half):
-            i = (my_i + j) % half
-            near_copy(p, i, my_i).start()
-            near_rest_copy(p, i, my_i).start()
-
-        @pl.when(jnp.logical_not(inner) & (p + 1 < last))
+        send_near(p)
+
+        @pl.when(p == 0)
         def _():
-            raw_copy(p + 1, my_k).start()
+            pl.semaphore_wait(known.at[1], 1)
+
+            @pl.when(inner)
+            def _():
+                tell(known.at[2], behind)
+
+            @pl.when(outer)
+            def _():
+                send_slots()
+
+        @pl.when(outer & (p < hops))
+        def _():
+            send_raw(p)
 
         return x
 
-    lax.fori_loop(0, parts, direct, 0)
-
-    def put_far(i, block):
-        far[i] = block
-
-    def put_far_rest(i, block):
-        far_rest[i] = block
-
-    fill(1, grad[:, columns_of(last)], scales_of(far_base), put_far, put_far_rest)
-    far_at = half + c0 * deep + my_k
-    for i in range(half):
-        far_copy(i, far_at).start()
-        far_rest_copy(i, far_at).start()
-
+    lax.fori_loop(0, chunks, direct, 0)
+
+    @pl.when(outer)
+    def _():
+        pl.semaphore_wait(known.at[2], 1)
+
+    far_scales = scales_of(far_base)
+
+    def directly_far(p, x):
+        columns = columns_of(p - hops)
+
+        def put(i, block):
+            far[i, :, columns] = block
+
+        def put_rest(i, block):
+            far_rest[i, :, columns] = block
+
+        fill(1, grad[:, columns_of(p)], far_scales, put, put_rest)
+        send_far(p)
+        return x
+
+    lax.fori_loop(hops, chunks, directly_far, 0)
     recv[my_i] = send[my_i]
     recv_rest[my_i] = send_rest[my_i]
     row_peak = jnp.max(jnp.abs(grad[...]).astype(jnp.float32), axis=1, keepdims=True)
@@ -552,8 +607,8 @@
 
     @pl.when(inner)
     def _():
+        came(slots_in, slot_recv)
         for k in range(deep):
-            slot_copy(k).wait_recv()
             spread(2 + k, lambda e: slots_in[k, pl.ds(e, 1), :], base)
 
     load.wait()
@@ -574,8 +629,8 @@
 
         @pl.when(inner)
         def _():
+            came(raw.at[:, :, columns], raw_recv.at[p])
             for k in range(deep):
-                raw_copy(p, k).wait_recv()
 
                 def put(i, block):
                     relay[i, k, :, columns] = block
@@ -584,57 +639,41 @@
                     relay_rest[i, k, :, columns] = block
 
                 fill(2 + k, raw[k, :, columns], near_scales, put, put_rest)
-            for j in range(1, half):
-                i = (my_i + j) % half
-                relay_copy(p, i, c0).start()
-                relay_rest_copy(p, i, c0).start()
+            send_relay(p)
             for k in range(deep):
                 recv[half + c0 * deep + k, :, columns] = relay[my_i, k, :, columns]
                 recv_rest[half + c0 * deep + k, :, columns] = relay_rest[my_i, k, :, columns]
-
-        for j in range(1, half):
-            i = (my_i + j) % half
-            near_copy(p, i, i).wait_recv()
-            near_rest_copy(p, i, i).wait_recv()
-        relay_copy(p, 0, 1 - c0).wait_recv()
-        relay_rest_copy(p, 0, 1 - c0).wait_recv()
-
-        @pl.when(jnp.logical_not(inner))
+            wait_chunk(p, half - 1 + deep)
+
+        @pl.when(outer)
         def _():
-            relay_copy(p, 0, c0).wait_recv()
-            relay_rest_copy(p, 0, c0).wait_recv()
+            wait_chunk(p, n_exp - 1)
 
         acc[...] = acc[...] + product_of(p)
         return x
 
-    lax.fori_loop(0, last, take, 0)
-
-    for j in range(1, half):
-        i = (my_i + j) % half
-        near_copy(last, i, i).wait_recv()
-        near_rest_copy(last, i, i).wait_recv()
-    for at in range(half, n_exp):
-        far_copy(0, at).wait_recv()
-        far_rest_copy(0, at).wait_recv()
-    acc[...] = acc[...] + product_of(last)
+    lax.fori_loop(0, hops, take, 0)
+
+    def take_tail(p, x):
+        wait_chunk(p, n_exp - 1)
+        acc[...] = acc[...] + product_of(p)
+        return x
+
+    lax.fori_loop(hops, chunks, take_tail, 0)
     hidden = acc[...] * back
     peak = jnp.max(jnp.max(jnp.abs(hidden), axis=0, keepdims=True), axis=1, keepdims=True)
     lane = lax.broadcasted_iota(jnp.int32, (1, LANES), 1)
     mine[...] = jnp.where(lane < experts, grad_peak, jnp.where(lane == experts + me, peak, 0.0))
-
-    def peak_copy(peer, slot, j):
-        return pltpu.make_async_remote_copy(
-            src_ref=mine, dst_ref=peaks_in.at[slot],
-            send_sem=peak_send.at[j], recv_sem=peak_recv.at[slot],
-            device_id=(peer // n_exp, peer % n_exp), device_id_type=MESH,
-        )
-
-    def peak_start(j, x):
-        peak_copy((here + j) % everyone, here, j).start()
-        return x
-
-    lax.fori_loop(1, everyone, peak_start, 0)
-
+    for k in range(n_exp // 2 - 1, -1, -1):
+        for c in (c0, 1 - c0):
+            for d in range(n_dp):
+                if k == 0 and c is c0 and d == 0:
+                    continue
+                pltpu.make_async_remote_copy(
+                    src_ref=mine, dst_ref=peaks_in.at[here], send_sem=peak_send, recv_sem=peak_recv,
+                    device_id=((my_dp + d) % n_dp, 2 * flip_bits(q0, k, n_exp // 2) + c), device_id_type=MESH,
+                ).start()
+    peaks_in[here] = mine[...]
     scaled = jnp.clip(acc[...] * back * own_hidden, -1.0, 1.0)
     for at in range(n_exp):
         if at < half:
@@ -645,53 +684,34 @@
         tail = n_exp * main + at * rest
         out_ref[block, first + main:first + capacity, :] = scaled[tail:tail + rest].astype(jnp.bfloat16)
 
-    def peak_fold(j, best):
-        peer = (here + j) % everyone
-        peak_copy(peer, peer, j).wait_recv()
-        return jnp.maximum(best, peaks_in[peer])
-
-    best_ref[...] = lax.fori_loop(1, everyone, peak_fold, mine[...])
-
-    def peak_finish(j, x):
-        peak_copy((here + j) % everyone, here, j).wait_send()
-        return x
-
-    lax.fori_loop(1, everyone, peak_finish, 0)
-    slot_copy(my_k).wait_send()
-
-    def drain(p, x):
-        for j in range(1, half):
-            i = (my_i + j) % half
-            near_copy(p, i, my_i).wait_send()
-            near_rest_copy(p, i, my_i).wait_send()
-
-        @pl.when(p < last)
-        def _():
-            raw_copy(p, my_k).wait_send()
-
-        @pl.when(inner & (p < last))
-        def _():
-            for j in range(1, half):
-                i = (my_i + j) % half
-                relay_copy(p, i, c0).wait_send()
-                relay_rest_copy(p, i, c0).wait_send()
-
-        return x
-
-    lax.fori_loop(0, parts, drain, 0)
-    for i in range(half):
-        far_copy(i, far_at).wait_send()
-        far_rest_copy(i, far_at).wait_send()
-
-
-def relay_finish(hist_g_ref, hist_h_ref, best_ref, out_ref, new_g_ref, new_h_ref, final_ref):
-    final_ref[...] = out_ref[...]
+    sent(slots.at[pl.ds(0, experts)], slot_send)
+    sent(grad.at[:, pl.ds(0, relayed)], raw_send)
+    sent(send.at[pl.ds(0, half - 1)], near_send)
+    sent(send_rest.at[pl.ds(0, half - 1)], near_rest_send)
+    sent(far, far_send)
+    sent(far_rest, far_rest_send)
+
+    @pl.when(inner)
+    def _():
+        sent(relay.at[pl.ds(0, half - 1)], relay_send)
+        sent(relay_rest.at[pl.ds(0, half - 1)], relay_rest_send)
+
+    others = peaks_in.at[pl.ds(0, everyone - 1)]
+    sent(others, peak_send)
+    came(others, peak_recv)
+    best_ref[...] = jnp.max(peaks_in[...], axis=0)
+
+
+def relay_finish(hist_g_ref, hist_h_ref, best_ref, out_ref, new_g_ref, new_h_ref, final_hbm, sem):
+    copy = pltpu.make_async_copy(out_ref, final_hbm, sem)
+    copy.start()
     keep = hist_g_ref.shape[0] - 1
     experts = hist_g_ref.shape[1]
     new_g_ref[0:keep, :] = hist_g_ref[1:keep + 1, :]
     new_g_ref[keep:keep + 1, :] = best_ref[0:1, 0:experts]
     new_h_ref[0:keep, :] = hist_h_ref[1:keep + 1, :]
     new_h_ref[keep:keep + 1, :] = best_ref[0:1, experts:2 * experts]
+    copy.wait()
 
 
 def by_relay(grad_out, expert_ids, down_weight, history_grad, history_hidden):
@@ -703,30 +723,32 @@
     rest = capacity - main
     units = down_weight.shape[1]
     half, deep = n_exp // 2, n_exp // 4
-    parts = RELAY_PARTS
-    span = width // parts
+    chunks = RELAY_CHUNKS
+    span = width // chunks
+    tail = RELAY_DIRECT * span
+    relayed = width - tail
     everyone = n_dp * n_exp
-    vmem = pl.BlockSpec(memory_space=pltpu.VMEM)
+    vmem, anywhere = pl.BlockSpec(memory_space=pltpu.VMEM), pl.BlockSpec(memory_space=pl.ANY)
     dma = pltpu.SemaphoreType.DMA
     bf16, f32 = jnp.bfloat16, jnp.float32
     out, best = pl.pallas_call(
-        functools.partial(relay_kernel, n_dp, n_exp, experts, capacity, parts),
-        out_shape=(
-            jax.ShapeDtypeStruct((2, half * capacity, units), bf16),
-            jax.ShapeDtypeStruct((1, LANES), f32),
-        ),
-        in_specs=[pl.BlockSpec(memory_space=pl.ANY), vmem, vmem, vmem, pl.BlockSpec(memory_space=pl.ANY)],
+        functools.partial(relay_kernel, n_dp, n_exp, experts, capacity, chunks),
+        out_shape=(pltpu.VMEM((2, half * capacity, units), bf16), pltpu.VMEM((1, LANES), f32)),
+        in_specs=[anywhere] * 5,
         out_specs=(vmem, vmem),
         scratch_shapes=[
             pltpu.VMEM((tokens, width), bf16),
-            pltpu.VMEM((deep, tokens, width), bf16),
+            pltpu.VMEM(expert_ids.shape[::-1], jnp.int32),
+            pltpu.VMEM(history_grad.shape, f32),
+            pltpu.VMEM(history_hidden.shape, f32),
+            pltpu.VMEM((deep, tokens, relayed), bf16),
             pltpu.VMEM((units, width), bf16),
             pltpu.VMEM((half, main, width), bf16),
             pltpu.VMEM((half, rest, width), bf16),
-            pltpu.VMEM((half, main, span), bf16),
-            pltpu.VMEM((half, rest, span), bf16),
-            pltpu.VMEM((half, deep, main, width), bf16),
-            pltpu.VMEM((half, deep, rest, width), bf16),
+            pltpu.VMEM((half, main, tail), bf16),
+            pltpu.VMEM((half, rest, tail), bf16),
+            pltpu.VMEM((half, deep, main, relayed), bf16),
+            pltpu.VMEM((half, deep, rest, relayed), bf16),
             pltpu.VMEM((n_exp, main, width), bf16),
             pltpu.VMEM((n_exp, rest, width), bf16),
             pltpu.VMEM((n_exp * rest, span), f32),
@@ -736,14 +758,12 @@
             pltpu.VMEM((2 + deep, half * capacity, tokens), bf16),
             pltpu.VMEM((1, LANES), f32),
             pltpu.VMEM((everyone, 1, LANES), f32),
-            dma, dma, dma((parts,)), dma((parts, deep)), dma, dma((deep,)),
-            dma((parts, half)), dma((parts, half)), dma((half,)), dma((half,)),
-            dma((parts, n_exp)), dma((parts, n_exp)),
-            dma((parts, half)), dma((parts, half)), dma((parts, 2)), dma((parts, 2)),
-            dma((everyone,)), dma((everyone,)),
+            dma((5,)), pltpu.SemaphoreType.REGULAR((3,)), dma, dma, dma, dma((relayed // span,)),
+            dma, dma, dma, dma, dma, dma,
+            dma((chunks,)), dma((chunks,)), dma, dma,
         ],
         compiler_params=pltpu.CompilerParams(
-            collective_id=1, has_side_effects=True, vmem_limit_bytes=60 * 1024 * 1024
+            collective_id=1, has_side_effects=True, vmem_limit_bytes=56 * 1024 * 1024
         ),
     )(grad_out, expert_ids.T, history_grad, history_hidden, down_weight)
     new_g, new_h, out = pl.pallas_call(
@@ -751,10 +771,12 @@
         out_shape=(
             jax.ShapeDtypeStruct(history_grad.shape, f32),
             jax.ShapeDtypeStruct(history_hidden.shape, f32),
-            jax.ShapeDtypeStruct(out.shape, out.dtype),
+            jax.ShapeDtypeStruct((2, half * capacity, units), bf16),
         ),
         in_specs=[vmem, vmem, vmem, vmem],
-        out_specs=(vmem, vmem, vmem),
+        out_specs=(vmem, vmem, anywhere),
+        scratch_shapes=[dma],
+        compiler_params=pltpu.CompilerParams(vmem_limit_bytes=4 * 1024 * 1024),
     )(history_grad, history_hidden, best, out)
     return out.reshape(1, 1, n_exp * capacity, units), new_g, new_h
 
@@ -762,8 +784,8 @@
 def fits_relay(tokens, width, experts, n_exp):
     capacity = tokens * 9 // 32
     return (
-        experts == n_exp and n_exp % 4 == 0 and experts % 8 == 0 and 2 * experts <= LANES
-        and tokens % LANES == 0 and width % (RELAY_PARTS * LANES) == 0
+        experts == n_exp and n_exp // 4 == 2 and experts % 8 == 0 and 2 * experts <= LANES
+        and tokens % LANES == 0 and width % (RELAY_CHUNKS * LANES) == 0
         and (n_exp // 2 * capacity) % 16 == 0 and (n_exp // 2 * (capacity % 16)) % 16 == 0
         and 0 < capacity % 16
     )

time: 59.3 us -> 51.3 us (0.87)
  Pallas kernels: 58.4 us -> 50.5 us
    pallas_call x1, Pallas kernels: 56.4 us -> 49 us  [by_relay(): pl.pallas_call(functools.partial(relay_kernel, n_dp, n_exp, experts, capa...]
where the time goes in v2:
time: 51.3 us; the launch traced here: 51.1 us
  Pallas kernels  50.5 us (98%)
  between operations  0.67 us (1%)
    pallas_call x1, Pallas kernels, by_relay(): pl.pallas_call(functools.partial(relay_kernel, n_dp, n_exp, experts, capa...  49 us
    pallas_call x1, Pallas kernels, by_relay(): pl.pallas_call(relay_finish, out_shape=(jax.ShapeDtypeStruct(history_grad...  1.42 us

profile of v2, /device:TPU:0, one launch (start us, length us, event | category | flops | bytes accessed | tf_op | source)
XLA Modules:
  0.0 51.1 jit_solution(14539884596501224149)
XLA Ops:
  0.6 0.0 copy-start.1
  0.6 0.0 copy-start
  0.7 49.0 %shard_map.76 = (bf16[2,144,1024]{2,1,0:T(8,128)(2,1)S(1)}, f32[1,128]{1,0:T(1,128)S(1)}) custom-call(bf16[128,3072]{1,0:T(8,128)(2,1)} %grad_hbm.1, s32[2,128]{1,0:T(2,128)} %bitcast.2, f32[8,8]{1,0:T(8,128)} %hist_g_ref.1, f32[8,8]{1,0:T(8,128)} %hist_h_ref.1, bf16[1,1024,3072]{2,1,0:T(8,128)(2,1)} %weight_hbm.1), custom_call_target="tpu_custom_call" | custom-call | tf_op jit(solution)/shard_map/pallas_call | solution.py:734
  49.7 0.0 copy-done.1
  49.7 0.0 copy-done
  49.7 1.4 %shard_map.77 = (f32[8,8]{1,0:T(8,128)}, f32[8,8]{1,0:T(8,128)}, bf16[2,144,1024]{2,1,0:T(8,128)(2,1)}) custom-call(f32[8,8]{1,0:T(8,128)S(1)} %copy-done, f32[8,8]{1,0:T(8,128)S(1)} %copy-done.1, f32[1,128]{1,0:T(1,128)S(1)} %get-tuple-element.8.best_ref, bf16[2,144,1024]{2,1,0:T(8,128)(2,1)S(1)} %get-tuple-element.9.out_ref), custom_call_target="tpu_custom_call" | custom-call | tf_op jit(solution)/shard_map/pallas_call | solution.py:769
Async XLA Ops:
  0.6 49.1 %copy-start.1 = (f32[8,8]{1,0:T(8,128)S(1)}, f32[8,8]{1,0:T(8,128)}, u32[]{:S(2)}) copy-start(f32[8,8]{1,0:T(8,128)} %hist_h_ref.1) | copy-start | bytes 772
  0.6 49.1 %copy-start = (f32[8,8]{1,0:T(8,128)S(1)}, f32[8,8]{1,0:T(8,128)}, u32[]{:S(2)}) copy-start(f32[8,8]{1,0:T(8,128)} %hist_g_ref.1) | copy-start | bytes 772
